TPU v7x, 32 devices: a whole 2x2x4 slice. The times are simulated.
32 devices in a mesh: gx: 8 (over z, x), gy: 4 (over y, core).
Axes of the slice: x: 2, y: 2, z: 4, core: 2. Of those that a mesh axis runs over, the one named last changes fastest.
Arguments:
- probe_seeds: int32 [4], replicated, may hold values from 0 to 1048575
- damping: float32 [512, 1024], P('gx', 'gy'), may hold values from 0.2 to 1
- coupling_x: float32 [512, 1024], P('gx', 'gy'), may hold values from 0.05 to 0.5
- coupling_y: float32 [512, 1024], P('gx', 'gy'), may hold values from 0.05 to 0.5
- sensor_count: int32 [8, 4], P('gx', 'gy'), may hold values from 1 to 256, as said below
- sensor_cells: int32 [8, 4, 256], P('gx', 'gy'), may hold values from 0 to 16383
- obs_weight: float32 [8, 4, 256, 256], P('gx', 'gy'), as said below
Outputs:
- solution: float32 [4, 512, 1024], P(None, 'gx', 'gy')
- trace_estimate: float32 [], replicated
Inputs may be any that keep to these rules, and one draw needn't show every extreme that they name: `sensor_count`: at most 256, and some block has exactly 256 in every draw; blocks near a few cluster centres are far busier than the rest. `sensor_cells`: cells within the block, numbered row by row. `obs_weight`: each block's matrix is symmetric positive definite.
All inputs are finite; a program needn't handle non-finite values.
Results may differ from a plain program's by a relative error of at most 0.0003.
Values sent between devices are 32-bit elements; how exact they have to be, the bound alone decides.
No kernel may reach another device: no remote copies, remote signals or barrier semaphores. Data moves between devices by JAX's collectives and lax.ppermute only.
A program may use at most 64 MiB of HBM per device.

v0:
```python
import jax
import jax.numpy as jnp
from jax import lax
from jax.sharding import PartitionSpec as P


def with_halo(cells, sides, width):
    for axis, dim in sides:
        count = lax.axis_size(axis)
        head = lax.slice_in_dim(cells, 0, width, axis=dim)
        tail = lax.slice_in_dim(cells, cells.shape[dim] - width, cells.shape[dim], axis=dim)
        cells = jnp.concatenate(
            [
                lax.ppermute(tail, axis, [(i, (i + 1) % count) for i in range(count)]),
                cells,
                lax.ppermute(head, axis, [((i + 1) % count, i) for i in range(count)]),
            ],
            axis=dim,
        )
    return cells


def shifted(value, axis, steps):
    count = lax.axis_size(axis)
    pairs = [(source, (source + steps) % count) for source in range(count)]
    return lax.ppermute(value, axis, pairs)


def rademacher(seeds, row_ids, col_ids):
    mixed = (
        seeds[:, None, None] * 668265261
        + row_ids[None, :, None] * 374761393
        + col_ids[None, None, :] * 1103515245
    )
    mixed = (mixed ^ mixed >> 16 & 65535) * 73244475
    mixed = (mixed ^ mixed >> 16 & 65535) * 73244475
    mixed = mixed ^ mixed >> 16 & 65535
    bit_value = mixed >> 7 & 1
    return (2 * bit_value - 1).astype(jnp.float32)


def apply_region(padded, damping, face_rows, face_cols):
    centre = padded[:, 1:-1, 1:-1]
    return (
        damping * centre
        + face_rows[1:] * (centre - padded[:, 2:, 1:-1])
        + face_rows[:-1] * (centre - padded[:, :-2, 1:-1])
        + face_cols[:, 1:] * (centre - padded[:, 1:-1, 2:])
        + face_cols[:, :-1] * (centre - padded[:, 1:-1, :-2])
    )


def rim_one(field):
    return with_halo(field, (("gx", 1), ("gy", 2)), 1)


def curvature(first, second):
    return lax.psum(jnp.sum(first * second, axis=(1, 2)), ("gx", "gy"))


def per_device(
    probe_seeds, damping, coupling_x, coupling_y, sensor_count, sensor_cells, obs_weight
):
    block_rows, block_cols = damping.shape
    row_ids = lax.axis_index("gx") * block_rows + jnp.arange(block_rows, dtype=jnp.int32)
    col_ids = lax.axis_index("gy") * block_cols + jnp.arange(block_cols, dtype=jnp.int32)
    probes = rademacher(probe_seeds, row_ids, col_ids)
    before_rows = shifted(coupling_x[-1:, :], "gx", 1)
    before_cols = shifted(coupling_y[:, -1:], "gy", 1)
    inner = (
        damping,
        jnp.concatenate([before_rows, coupling_x], 0),
        jnp.concatenate([before_cols, coupling_y], 1),
    )
    count = sensor_count[0, 0]
    cell_ids = sensor_cells[0, 0]
    weight = obs_weight[0, 0]
    mask = (jnp.arange(weight.shape[0]) < count).astype(jnp.float32)

    def observe(field):
        flat = field.reshape(field.shape[0], -1)
        sampled = jnp.take(flat, cell_ids, axis=1) * mask
        weighted = jnp.dot(sampled, weight, precision=lax.Precision.HIGHEST)
        weighted = weighted * mask
        return jnp.zeros_like(flat).at[:, cell_ids].add(weighted).reshape(field.shape)

    def operator_twice(field):
        once = apply_region(rim_one(field), *inner)
        return apply_region(rim_one(once), *inner)

    def hessian(field):
        return operator_twice(field) + observe(field)

    cells_total = block_rows * block_cols * lax.axis_size("gx") * lax.axis_size("gy")
    norm_start = jnp.full((probes.shape[0],), float(cells_total), jnp.float32)
    image = hessian(probes)
    first_step = norm_start / curvature(probes, image)
    solution = first_step[:, None, None] * probes
    residual = probes - first_step[:, None, None] * image
    residual_image = hessian(residual)
    norm_next, product = lax.psum(
        (
            jnp.sum(residual * residual, axis=(1, 2)),
            jnp.sum(residual * residual_image, axis=(1, 2)),
        ),
        ("gx", "gy"),
    )
    ratio = norm_next / norm_start
    direction = residual + ratio[:, None, None] * probes
    second_step = norm_next / (product - ratio * norm_next / first_step)
    solution = solution + second_step[:, None, None] * direction
    total = lax.psum(jnp.sum(probes * solution), ("gx", "gy"))
    return (solution, total / probes.shape[0])


def solution(mesh):
    placed = (
        P(),
        P("gx", "gy"),
        P("gx", "gy"),
        P("gx", "gy"),
        P("gx", "gy"),
        P("gx", "gy", None),
        P("gx", "gy", None, None),
    )
    return jax.shard_map(
        per_device,
        mesh=mesh,
        in_specs=placed,
        out_specs=(P(None, "gx", "gy"), P()),
        check_vma=False,
    )
```

profile of v0, /device:TPU:0, one launch (start us, length us, event | category | flops | bytes accessed | tf_op | source)
XLA Modules:
  0.0 211.1 jit_solution(12646196828088814270)
XLA Ops:
  1.8 6.1 %collective-permute-start = (f32[4,1,256]{2,1,0:T(1,128)S(1)}, f32[4,1,256]{2,1,0:T(1,128)S(1)}, u32[]{:S(2)}, u32[]{:S(2)}) collective-permute-start(f32[4,1,256]{2,1,0:T(1,128)S(1)} %get-tuple-element.26), channel_id=1, source_target_pairs={{4,0},{8,4},{12,8},{16,12},{20,16},{24,20},{28,24},{0,28},{5,1},{9... | collective-permute-start | bytes 12296 | tf_op jit(solution)/shard_map/ppermute | solution.py:16
  11.9 5.1 %copy.25 = f32[4,16384]{0,1:T(8,128)} copy(f32[4,16384]{1,0:T(4,128)S(1)} %add_convert_fusion) | data formatting | bytes 524288 | tf_op jit(solution)/shard_map/convert_element_type | solution.py:39
  16.9 4.1 %gather_fusion = f32[256,4]{1,0:T(8,128)S(1)} fusion(f32[4,16384]{0,1:T(8,128)} %copy.25, s32[1024]{0:T(1024)S(1)} %pad_clamp_fusion), kind=kCustom, calls=%fused_computation.clone | custom fusion | bytes 9216 | tf_op jit(solution)/shard_map/jit(_take)/gather | solution.py:82
  21.4 1.7 collective-permute-start.5
  23.2 2.7 %collective-permute-done.5 = f32[4,66,1]{2,1,0:T(8,128)S(1)} collective-permute-done((f32[4,66,1]{2,1,0:T(8,128)S(1)}, f32[4,66,1]{2,1,0:T(8,128)S(1)}, u32[]{:S(2)}, u32[]{:S(2)}) %collective-permute-start.5) | collective-permute-done | bytes 1088 | tf_op jit(solution)/shard_map/ppermute | solution.py:14
  26.9 4.8 %collective-permute-start.6 = (f32[4,1,256]{2,1,0:T(1,128)S(1)}, f32[4,1,256]{2,1,0:T(1,128)S(1)}, u32[]{:S(2)}, u32[]{:S(2)}) collective-permute-start(f32[4,1,256]{2,1,0:T(1,128)S(1)} %get-tuple-element.24), channel_id=1, source_target_pairs={{4,0},{8,4},{12,8},{16,12},{20,16},{24,20},{28,24},{0,28},{5,1},{9... | collective-permute-start | bytes 12296 | tf_op jit(solution)/shard_map/ppermute | solution.py:16
  33.0 5.0 %collective-permute-done.7 = f32[4,1,256]{2,1,0:T(1,128)S(1)} collective-permute-done((f32[4,1,256]{2,1,0:T(1,128)S(1)}, f32[4,1,256]{2,1,0:T(1,128)S(1)}, u32[]{:S(2)}, u32[]{:S(2)}) %collective-permute-start.7) | collective-permute-done | bytes 4128 | tf_op jit(solution)/shard_map/ppermute | solution.py:14
  38.2 1.7 collective-permute-start.8
  40.1 5.1 %scatter_custom_fusion = f32[4,16384]{0,1:T(8,128)} fusion(s32[256]{0:T(256)S(1)} %bitcast.37, f32[256,4]{1,0:T(8,128)S(1)} %copy.27, f32[]{:T(128)} %constant.53.clone.1), kind=kCustom, calls=%fused_computation.6 | custom fusion | flops 1024 | bytes 262148 | tf_op jit(solution)/shard_map/scatter-add | solution.py:85
  45.2 5.2 %copy.28 = f32[4,64,256]{2,1,0:T(8,128)S(1)} copy(f32[4,64,256]{0,2,1:T(8,128)} %bitcast.31) | data formatting | bytes 524288 | tf_op jit(solution)/shard_map/reshape | solution.py:85
  51.0 36.9 %psum.28 = f32[4]{0:T(128)S(1)} all-reduce(f32[4]{0:T(128)S(1)} %get-tuple-element.9), channel_id=1, replica_groups=mesh['gx'=8,'gy'=4] {'gx','gy'}, use_global_device_ids=true, to_apply=%region_2.4 | all-reduce | flops 4 | bytes 32 | tf_op jit(solution)/shard_map/psum | solution.py:58
  88.2 4.0 %collective-permute-start.10 = (f32[4,1,256]{2,1,0:T(1,128)S(1)}, f32[4,1,256]{2,1,0:T(1,128)S(1)}, u32[]{:S(2)}, u32[]{:S(2)}) collective-permute-start(f32[4,1,256]{2,1,0:T(1,128)S(1)} %get-tuple-element.22), channel_id=1, source_target_pairs={{4,0},{8,4},{12,8},{16,12},{20,16},{24,20},{28,24},{0,28},{5,1},{9... | collective-permute-start | bytes 12296 | tf_op jit(solution)/shard_map/ppermute | solution.py:16
  92.2 1.3 collective-permute-done.10
  93.6 5.0 %collective-permute-done.11 = f32[4,1,256]{2,1,0:T(1,128)S(1)} collective-permute-done((f32[4,1,256]{2,1,0:T(1,128)S(1)}, f32[4,1,256]{2,1,0:T(1,128)S(1)}, u32[]{:S(2)}, u32[]{:S(2)}) %collective-permute-start.11) | collective-permute-done | bytes 4128 | tf_op jit(solution)/shard_map/ppermute | solution.py:14
  98.7 1.7 collective-permute-start.12
  100.5 2.8 %collective-permute-done.13 = f32[4,66,1]{2,1,0:T(8,128)S(1)} collective-permute-done((f32[4,66,1]{2,1,0:T(8,128)S(1)}, f32[4,66,1]{2,1,0:T(8,128)S(1)}, u32[]{:S(2)}, u32[]{:S(2)}) %collective-permute-start.13) | collective-permute-done | bytes 1088 | tf_op jit(solution)/shard_map/ppermute | solution.py:14
  104.3 2.0 collective-permute-start.15
  106.3 4.6 %copy.29 = f32[4,64,256]{0,2,1:T(8,128)} copy(f32[4,64,256]{2,1,0:T(8,128)S(1)} %get-tuple-element.8) | data formatting | bytes 524288 | tf_op jit(solution)/shard_map/sub | solution.py:99
  111.0 4.1 %gather_fusion.1 = f32[256,4]{1,0:T(8,128)S(1)} fusion(f32[4,16384]{0,1:T(8,128)} %bitcast.32, s32[1024]{0:T(1024)S(1)} %pad_clamp_fusion), kind=kCustom, calls=%fused_computation.1.clone | custom fusion | bytes 9216 | tf_op jit(solution)/shard_map/jit(_take)/gather | solution.py:82
  117.5 5.1 %scatter_custom_fusion.1 = f32[4,16384]{0,1:T(8,128)} fusion(s32[256]{0:T(256)S(1)} %bitcast.38, f32[256,4]{1,0:T(8,128)S(1)} %copy.31, f32[]{:T(128)} %constant.53.clone.1), kind=kCustom, calls=%fused_computation.4 | custom fusion | flops 1024 | bytes 262148 | tf_op jit(solution)/shard_map/scatter-add | solution.py:85
  122.6 5.2 %copy.32 = f32[4,64,256]{2,1,0:T(8,128)S(1)} copy(f32[4,64,256]{0,2,1:T(8,128)} %bitcast.30) | data formatting | bytes 524288 | tf_op jit(solution)/shard_map/reshape | solution.py:85
  128.2 38.3 %all-reduce = (f32[4]{0:T(128)S(1)}, f32[4]{0:T(128)S(1)}) all-reduce(f32[4]{0:T(128)S(1)} %get-tuple-element.7, f32[4]{0:T(128)S(1)} %fusion.17), channel_id=1, replica_groups=mesh['gx'=8,'gy'=4] {'gx','gy'}, use_global_device_ids=true, to_apply=%region_4.6 | all-reduce | flops 8 | bytes 64 | tf_op jit(solution)/shard_map/psum | solution.py:101
  166.5 1.6 multiply_reduce_fusion
  168.1 41.2 %psum.31 = f32[]{:T(128)} all-reduce(f32[]{:T(128)} %get-tuple-element.5), channel_id=1, replica_groups=mesh['gx'=8,'gy'=4] {'gx','gy'}, use_global_device_ids=true, to_apply=%region_9.11 | all-reduce | flops 1 | bytes 8 | tf_op jit(solution)/shard_map/psum | solution.py:112
  (76 shorter events, 12.3 us)
Async XLA Ops:
  0.6 31.1 %copy-start = (f32[1,1,256,256]{3,2,1,0:T(8,128)S(1)}, f32[1,1,256,256]{3,2,1,0:T(8,128)}, u32[]{:S(2)}) copy-start(f32[1,1,256,256]{3,2,1,0:T(8,128)} %param.15) | copy-start | bytes 786436
  0.6 20.5 %copy-start.1 = (f32[64,256]{1,0:T(8,128)S(1)}, f32[64,256]{1,0:T(8,128)}, u32[]{:S(2)}) copy-start(f32[64,256]{1,0:T(8,128)} %param.12) | copy-start | bytes 196612
  0.7 22.6 %copy-start.2 = (f32[64,256]{1,0:T(8,128)S(1)}, f32[64,256]{1,0:T(8,128)}, u32[]{:S(2)}) copy-start(f32[64,256]{1,0:T(8,128)} %param.11) | copy-start | bytes 196612
  0.7 39.3 %copy-start.4 = (s32[1,1,256]{2,1,0:T(1,128)S(1)}, s32[1,1,256]{2,1,0:T(1,128)}, u32[]{:S(2)}) copy-start(s32[1,1,256]{2,1,0:T(1,128)} %param.14) | copy-start | bytes 3076
  0.7 25.9 %copy-start.3 = (f32[64,256]{1,0:T(8,128)S(1)}, f32[64,256]{1,0:T(8,128)}, u32[]{:S(2)}) copy-start(f32[64,256]{1,0:T(8,128)} %param.10) | copy-start | bytes 196612
  1.8 19.5 %collective-permute-start = (f32[4,1,256]{2,1,0:T(1,128)S(1)}, f32[4,1,256]{2,1,0:T(1,128)S(1)}, u32[]{:S(2)}, u32[]{:S(2)}) collective-permute-start(f32[4,1,256]{2,1,0:T(1,128)S(1)} %get-tuple-element.26), channel_id=1, source_target_pairs={{4,0},{8,4},{12,8},{16,12},{20,16},{24,20},{28,24},{0,28},{5,1},{9... | collective-permute-start | bytes 12296 | tf_op jit(solution)/shard_map/ppermute | solution.py:16
  7.8 13.4 %collective-permute-start.2 = (f32[4,1,256]{2,1,0:T(1,128)S(1)}, f32[4,1,256]{2,1,0:T(1,128)S(1)}, u32[]{:S(2)}, u32[]{:S(2)}) collective-permute-start(f32[4,1,256]{2,1,0:T(1,128)S(1)} %get-tuple-element.25), channel_id=1, source_target_pairs={{0,4},{4,8},{8,12},{12,16},{16,20},{20,24},{24,28},{28,0},{1,5},{5... | collective-permute-start | bytes 12296 | tf_op jit(solution)/shard_map/ppermute | solution.py:14
  8.6 12.5 %collective-permute-start.4 = (f32[64,1]{1,0:T(8,128)S(1)}, f32[64,1]{1,0:T(8,128)S(1)}, u32[]{:S(2)}, u32[]{:S(2)}) collective-permute-start(f32[64,1]{1,0:T(8,128)S(1)} %slice.138), channel_id=1, source_target_pairs={{0,1},{1,2},{2,3},{3,0},{4,5},{5,6},{6,7},{7,4},{8,9},{9,10},{10,1... | collective-permute-start | bytes 776 | tf_op jit(solution)/shard_map/ppermute | solution.py:26
  9.4 13.9 %collective-permute-start.1 = (f32[1,256]{1,0:T(1,128)S(1)}, f32[1,256]{1,0:T(1,128)S(1)}, u32[]{:S(2)}, u32[]{:S(2)}) collective-permute-start(f32[1,256]{1,0:T(1,128)S(1)} %slice.132), channel_id=1, source_target_pairs={{0,4},{4,8},{8,12},{12,16},{16,20},{20,24},{24,28},{28,0},{1,5},{5... | collective-permute-start | bytes 3080 | tf_op jit(solution)/shard_map/ppermute | solution.py:26
  21.4 4.6 %collective-permute-start.5 = (f32[4,66,1]{2,1,0:T(8,128)S(1)}, f32[4,66,1]{2,1,0:T(8,128)S(1)}, u32[]{:S(2)}, u32[]{:S(2)}) collective-permute-start(f32[4,66,1]{2,1,0:T(8,128)S(1)} %get-tuple-element.18), channel_id=1, source_target_pairs={{0,1},{1,2},{2,3},{3,0},{4,5},{5,6},{6,7},{7,4},{8,9},{9,10},{10,1... | collective-permute-start | bytes 3176 | tf_op jit(solution)/shard_map/ppermute | solution.py:14
  23.1 3.6 %collective-permute-start.3 = (f32[4,66,1]{2,1,0:T(8,128)S(1)}, f32[4,66,1]{2,1,0:T(8,128)S(1)}, u32[]{:S(2)}, u32[]{:S(2)}) collective-permute-start(f32[4,66,1]{2,1,0:T(8,128)S(1)} %get-tuple-element.17), channel_id=1, source_target_pairs={{1,0},{2,1},{3,2},{0,3},{5,4},{6,5},{7,6},{4,7},{9,8},{10,9},{11,1... | collective-permute-start | bytes 3176 | tf_op jit(solution)/shard_map/ppermute | solution.py:16
  26.9 6.1 %collective-permute-start.6 = (f32[4,1,256]{2,1,0:T(1,128)S(1)}, f32[4,1,256]{2,1,0:T(1,128)S(1)}, u32[]{:S(2)}, u32[]{:S(2)}) collective-permute-start(f32[4,1,256]{2,1,0:T(1,128)S(1)} %get-tuple-element.24), channel_id=1, source_target_pairs={{4,0},{8,4},{12,8},{16,12},{20,16},{24,20},{28,24},{0,28},{5,1},{9... | collective-permute-start | bytes 12296 | tf_op jit(solution)/shard_map/ppermute | solution.py:16
  31.7 6.3 %collective-permute-start.7 = (f32[4,1,256]{2,1,0:T(1,128)S(1)}, f32[4,1,256]{2,1,0:T(1,128)S(1)}, u32[]{:S(2)}, u32[]{:S(2)}) collective-permute-start(f32[4,1,256]{2,1,0:T(1,128)S(1)} %get-tuple-element.23), channel_id=1, source_target_pairs={{0,4},{4,8},{8,12},{12,16},{16,20},{20,24},{24,28},{28,0},{1,5},{5... | collective-permute-start | bytes 12296 | tf_op jit(solution)/shard_map/ppermute | solution.py:14
  38.1 12.3 %collective-permute-start.9 = (f32[4,66,1]{2,1,0:T(8,128)S(1)}, f32[4,66,1]{2,1,0:T(8,128)S(1)}, u32[]{:S(2)}, u32[]{:S(2)}) collective-permute-start(f32[4,66,1]{2,1,0:T(8,128)S(1)} %get-tuple-element.16), channel_id=1, source_target_pairs={{0,1},{1,2},{2,3},{3,0},{4,5},{5,6},{6,7},{7,4},{8,9},{9,10},{10,1... | collective-permute-start | bytes 3176 | tf_op jit(solution)/shard_map/ppermute | solution.py:14
  38.2 12.3 %collective-permute-start.8 = (f32[4,66,1]{2,1,0:T(8,128)S(1)}, f32[4,66,1]{2,1,0:T(8,128)S(1)}, u32[]{:S(2)}, u32[]{:S(2)}) collective-permute-start(f32[4,66,1]{2,1,0:T(8,128)S(1)} %get-tuple-element.15), channel_id=1, source_target_pairs={{1,0},{2,1},{3,2},{0,3},{5,4},{6,5},{7,6},{4,7},{9,8},{10,9},{11,1... | collective-permute-start | bytes 3176 | tf_op jit(solution)/shard_map/ppermute | solution.py:16
  88.2 5.4 %collective-permute-start.10 = (f32[4,1,256]{2,1,0:T(1,128)S(1)}, f32[4,1,256]{2,1,0:T(1,128)S(1)}, u32[]{:S(2)}, u32[]{:S(2)}) collective-permute-start(f32[4,1,256]{2,1,0:T(1,128)S(1)} %get-tuple-element.22), channel_id=1, source_target_pairs={{4,0},{8,4},{12,8},{16,12},{20,16},{24,20},{28,24},{0,28},{5,1},{9... | collective-permute-start | bytes 12296 | tf_op jit(solution)/shard_map/ppermute | solution.py:16
  92.2 6.3 %collective-permute-start.11 = (f32[4,1,256]{2,1,0:T(1,128)S(1)}, f32[4,1,256]{2,1,0:T(1,128)S(1)}, u32[]{:S(2)}, u32[]{:S(2)}) collective-permute-start(f32[4,1,256]{2,1,0:T(1,128)S(1)} %get-tuple-element.21), channel_id=1, source_target_pairs={{0,4},{4,8},{8,12},{12,16},{16,20},{20,24},{24,28},{28,0},{1,5},{5... | collective-permute-start | bytes 12296 | tf_op jit(solution)/shard_map/ppermute | solution.py:14
  98.7 4.6 %collective-permute-start.13 = (f32[4,66,1]{2,1,0:T(8,128)S(1)}, f32[4,66,1]{2,1,0:T(8,128)S(1)}, u32[]{:S(2)}, u32[]{:S(2)}) collective-permute-start(f32[4,66,1]{2,1,0:T(8,128)S(1)} %get-tuple-element.14), channel_id=1, source_target_pairs={{0,1},{1,2},{2,3},{3,0},{4,5},{5,6},{6,7},{7,4},{8,9},{9,10},{10,1... | collective-permute-start | bytes 3176 | tf_op jit(solution)/shard_map/ppermute | solution.py:14
  98.7 5.2 %collective-permute-start.12 = (f32[4,66,1]{2,1,0:T(8,128)S(1)}, f32[4,66,1]{2,1,0:T(8,128)S(1)}, u32[]{:S(2)}, u32[]{:S(2)}) collective-permute-start(f32[4,66,1]{2,1,0:T(8,128)S(1)} %get-tuple-element.13), channel_id=1, source_target_pairs={{1,0},{2,1},{3,2},{0,3},{5,4},{6,5},{7,6},{4,7},{9,8},{10,9},{11,1... | collective-permute-start | bytes 3176 | tf_op jit(solution)/shard_map/ppermute | solution.py:16
  104.3 10.9 %collective-permute-start.14 = (f32[4,1,256]{2,1,0:T(1,128)S(1)}, f32[4,1,256]{2,1,0:T(1,128)S(1)}, u32[]{:S(2)}, u32[]{:S(2)}) collective-permute-start(f32[4,1,256]{2,1,0:T(1,128)S(1)} %get-tuple-element.20), channel_id=1, source_target_pairs={{4,0},{8,4},{12,8},{16,12},{20,16},{24,20},{28,24},{0,28},{5,1},{9... | collective-permute-start | bytes 12296 | tf_op jit(solution)/shard_map/ppermute | solution.py:16
  104.3 10.8 %collective-permute-start.15 = (f32[4,1,256]{2,1,0:T(1,128)S(1)}, f32[4,1,256]{2,1,0:T(1,128)S(1)}, u32[]{:S(2)}, u32[]{:S(2)}) collective-permute-start(f32[4,1,256]{2,1,0:T(1,128)S(1)} %get-tuple-element.19), channel_id=1, source_target_pairs={{0,4},{4,8},{8,12},{12,16},{16,20},{20,24},{24,28},{28,0},{1,5},{5... | collective-permute-start | bytes 12296 | tf_op jit(solution)/shard_map/ppermute | solution.py:14
  115.3 12.6 %collective-permute-start.17 = (f32[4,66,1]{2,1,0:T(8,128)S(1)}, f32[4,66,1]{2,1,0:T(8,128)S(1)}, u32[]{:S(2)}, u32[]{:S(2)}) collective-permute-start(f32[4,66,1]{2,1,0:T(8,128)S(1)} %get-tuple-element.12), channel_id=1, source_target_pairs={{0,1},{1,2},{2,3},{3,0},{4,5},{5,6},{6,7},{7,4},{8,9},{9,10},{10,1... | collective-permute-start | bytes 3176 | tf_op jit(solution)/shard_map/ppermute | solution.py:14
  115.8 12.1 %collective-permute-start.16 = (f32[4,66,1]{2,1,0:T(8,128)S(1)}, f32[4,66,1]{2,1,0:T(8,128)S(1)}, u32[]{:S(2)}, u32[]{:S(2)}) collective-permute-start(f32[4,66,1]{2,1,0:T(8,128)S(1)} %get-tuple-element.11), channel_id=1, source_target_pairs={{1,0},{2,1},{3,2},{0,3},{5,4},{6,5},{7,6},{4,7},{9,8},{10,9},{11,1... | collective-permute-start | bytes 3176 | tf_op jit(solution)/shard_map/ppermute | solution.py:16
where the time goes:
time: 212 us; the launch traced here: 211 us
  blocking collectives  116 us (55%)
  local copies, waits for them, and re-layouts  31 us (15%)
  starting transfers between devices  24.2 us (11%)
  waiting for transfers between devices  19.3 us (9%)
  other arithmetic  16.5 us (8%)
  between operations  3.4 us (2%)
    psum x1, blocking collectives, per_device(): total = lax.psum(jnp.sum(probes * solution), ('gx', 'gy'))  41.2 us
    psum x1, blocking collectives, per_device(): lax.psum((jnp.sum(residual * residual, axis=(1, 2)), jnp.sum(residual * r...  38.3 us
    psum x1, blocking collectives, curvature(): return lax.psum(jnp.sum(first * second, axis=(1, 2)), ('gx', 'gy'))  36.9 us
    ppermute x8, starting transfers between devices, with_halo(): lax.ppermute(head, axis, [((i + 1) % count, i) for i in range(count)])  19.9 us
    ppermute x8, waiting for transfers between devices, with_halo(): lax.ppermute(tail, axis, [(i, (i + 1) % count) for i in range(count)])  15.5 us
    reshape x2, local copies, waits for them, and re-layouts, observe(): jnp.zeros_like(flat).at[:, cell_ids].add(weighted).reshape(field.shape)  10.5 us
    scatter-add x2, other arithmetic, observe(): jnp.zeros_like(flat).at[:, cell_ids].add(weighted).reshape(field.shape)  10.3 us
    gather x4, local copies, waits for them, and re-layouts, observe(): sampled = jnp.take(flat, cell_ids, axis=1) * mask  8.35 us
  transfers between devices with their start and end apart: 18, of which 8 were waited for; matrix products, arithmetic and copies ran while one was open for 20% of the time, Pallas kernels for 0%

commit v1 on v0

--- a/solution.py
+++ b/solution.py
@@ -99,11 +99,14 @@
     residual = probes - first_step[:, None, None] * image
     residual_image = hessian(residual)
     norm_next, product = lax.psum(
-        (
-            jnp.sum(residual * residual, axis=(1, 2)),
-            jnp.sum(residual * residual_image, axis=(1, 2)),
+        lax.psum(
+            (
+                jnp.sum(residual * residual, axis=(1, 2)),
+                jnp.sum(residual * residual_image, axis=(1, 2)),
+            ),
+            "gx",
         ),
-        ("gx", "gy"),
+        "gy",
     )
     ratio = norm_next / norm_start
     direction = residual + ratio[:, None, None] * probes

time: 212 us -> 196 us (0.925)
  blocking collectives: 116 us -> 99.4 us
    psum x1, blocking collectives: 38.3 us -> 19.9 us  [per_device(): lax.psum((jnp.sum(residual * residual, axis=(1, 2)), jnp.sum(residual * r...]
    psum x0 -> x1, blocking collectives: none -> 5.65 us  [per_device(): lax.psum(lax.psum((jnp.sum(residual * residual, axis=(1, 2)), jnp.sum(res...]
    psum x1, blocking collectives: 41.2 us -> 37 us  [per_device(): total = lax.psum(jnp.sum(probes * solution), ('gx', 'gy'))]
  transfers between devices with their start and end apart: 18 -> 18, of which waited for: 8 -> 8; matrix products, arithmetic and copies ran while one was open for 20% -> 22% of each run, Pallas kernels for 0% -> 0%
where the time goes in v1:
time: 196 us; the launch traced here: 194 us
  blocking collectives  99.4 us (51%)
  local copies, waits for them, and re-layouts  31 us (16%)
  starting transfers between devices  24.2 us (12%)
  waiting for transfers between devices  19.3 us (10%)
  other arithmetic  16.5 us (8%)
  between operations  3.4 us (2%)
    psum x1, blocking collectives, per_device(): total = lax.psum(jnp.sum(probes * solution), ('gx', 'gy'))  37 us
    psum x1, blocking collectives, curvature(): return lax.psum(jnp.sum(first * second, axis=(1, 2)), ('gx', 'gy'))  36.9 us
    ppermute x8, starting transfers between devices, with_halo(): lax.ppermute(head, axis, [((i + 1) % count, i) for i in range(count)])  19.9 us
    psum x1, blocking collectives, per_device(): lax.psum((jnp.sum(residual * residual, axis=(1, 2)), jnp.sum(residual * r...  19.9 us
    ppermute x8, waiting for transfers between devices, with_halo(): lax.ppermute(tail, axis, [(i, (i + 1) % count) for i in range(count)])  15.5 us
    reshape x2, local copies, waits for them, and re-layouts, observe(): jnp.zeros_like(flat).at[:, cell_ids].add(weighted).reshape(field.shape)  10.5 us
    scatter-add x2, other arithmetic, observe(): jnp.zeros_like(flat).at[:, cell_ids].add(weighted).reshape(field.shape)  10.3 us
    gather x4, local copies, waits for them, and re-layouts, observe(): sampled = jnp.take(flat, cell_ids, axis=1) * mask  8.35 us
  transfers between devices with their start and end apart: 18, of which 8 were waited for; matrix products, arithmetic and copies ran while one was open for 22% of the time, Pallas kernels for 0%

profile of v1, /device:TPU:0, one launch (start us, length us, event | category | flops | bytes accessed | tf_op | source)
XLA Modules:
  0.0 194.2 jit_solution(14259969784255963918)
XLA Ops:
  1.8 6.1 %collective-permute-start = (f32[4,1,256]{2,1,0:T(1,128)S(1)}, f32[4,1,256]{2,1,0:T(1,128)S(1)}, u32[]{:S(2)}, u32[]{:S(2)}) collective-permute-start(f32[4,1,256]{2,1,0:T(1,128)S(1)} %get-tuple-element.28), channel_id=1, source_target_pairs={{4,0},{8,4},{12,8},{16,12},{20,16},{24,20},{28,24},{0,28},{5,1},{9... | collective-permute-start | bytes 12296 | tf_op jit(solution)/shard_map/ppermute | solution.py:16
  11.9 5.1 %copy.25 = f32[4,16384]{0,1:T(8,128)} copy(f32[4,16384]{1,0:T(4,128)S(1)} %add_convert_fusion) | data formatting | bytes 524288 | tf_op jit(solution)/shard_map/convert_element_type | solution.py:39
  16.9 4.1 %gather_fusion = f32[256,4]{1,0:T(8,128)S(1)} fusion(f32[4,16384]{0,1:T(8,128)} %copy.25, s32[1024]{0:T(1024)S(1)} %pad_clamp_fusion), kind=kCustom, calls=%fused_computation.clone | custom fusion | bytes 9216 | tf_op jit(solution)/shard_map/jit(_take)/gather | solution.py:82
  21.4 1.7 collective-permute-start.5
  23.3 2.7 %collective-permute-done.5 = f32[4,66,1]{2,1,0:T(8,128)S(1)} collective-permute-done((f32[4,66,1]{2,1,0:T(8,128)S(1)}, f32[4,66,1]{2,1,0:T(8,128)S(1)}, u32[]{:S(2)}, u32[]{:S(2)}) %collective-permute-start.5) | collective-permute-done | bytes 1088 | tf_op jit(solution)/shard_map/ppermute | solution.py:14
  26.9 4.8 %collective-permute-start.6 = (f32[4,1,256]{2,1,0:T(1,128)S(1)}, f32[4,1,256]{2,1,0:T(1,128)S(1)}, u32[]{:S(2)}, u32[]{:S(2)}) collective-permute-start(f32[4,1,256]{2,1,0:T(1,128)S(1)} %get-tuple-element.26), channel_id=1, source_target_pairs={{4,0},{8,4},{12,8},{16,12},{20,16},{24,20},{28,24},{0,28},{5,1},{9... | collective-permute-start | bytes 12296 | tf_op jit(solution)/shard_map/ppermute | solution.py:16
  33.0 5.0 %collective-permute-done.7 = f32[4,1,256]{2,1,0:T(1,128)S(1)} collective-permute-done((f32[4,1,256]{2,1,0:T(1,128)S(1)}, f32[4,1,256]{2,1,0:T(1,128)S(1)}, u32[]{:S(2)}, u32[]{:S(2)}) %collective-permute-start.7) | collective-permute-done | bytes 4128 | tf_op jit(solution)/shard_map/ppermute | solution.py:14
  38.2 1.7 collective-permute-start.8
  40.1 5.1 %scatter_custom_fusion = f32[4,16384]{0,1:T(8,128)} fusion(s32[256]{0:T(256)S(1)} %bitcast.37, f32[256,4]{1,0:T(8,128)S(1)} %copy.27, f32[]{:T(128)} %constant.53.clone.1), kind=kCustom, calls=%fused_computation.6 | custom fusion | flops 1024 | bytes 262148 | tf_op jit(solution)/shard_map/scatter-add | solution.py:85
  45.2 5.2 %copy.28 = f32[4,64,256]{2,1,0:T(8,128)S(1)} copy(f32[4,64,256]{0,2,1:T(8,128)} %bitcast.31) | data formatting | bytes 524288 | tf_op jit(solution)/shard_map/reshape | solution.py:85
  51.0 36.9 %psum.42 = f32[4]{0:T(128)S(1)} all-reduce(f32[4]{0:T(128)S(1)} %get-tuple-element.11), channel_id=1, replica_groups=mesh['gx'=8,'gy'=4] {'gx','gy'}, use_global_device_ids=true, to_apply=%region_2.4 | all-reduce | flops 4 | bytes 32 | tf_op jit(solution)/shard_map/psum | solution.py:58
  88.2 4.0 %collective-permute-start.10 = (f32[4,1,256]{2,1,0:T(1,128)S(1)}, f32[4,1,256]{2,1,0:T(1,128)S(1)}, u32[]{:S(2)}, u32[]{:S(2)}) collective-permute-start(f32[4,1,256]{2,1,0:T(1,128)S(1)} %get-tuple-element.24), channel_id=1, source_target_pairs={{4,0},{8,4},{12,8},{16,12},{20,16},{24,20},{28,24},{0,28},{5,1},{9... | collective-permute-start | bytes 12296 | tf_op jit(solution)/shard_map/ppermute | solution.py:16
  93.6 5.0 %collective-permute-done.11 = f32[4,1,256]{2,1,0:T(1,128)S(1)} collective-permute-done((f32[4,1,256]{2,1,0:T(1,128)S(1)}, f32[4,1,256]{2,1,0:T(1,128)S(1)}, u32[]{:S(2)}, u32[]{:S(2)}) %collective-permute-start.11) | collective-permute-done | bytes 4128 | tf_op jit(solution)/shard_map/ppermute | solution.py:14
  98.8 1.7 collective-permute-start.12
  100.5 2.8 %collective-permute-done.13 = f32[4,66,1]{2,1,0:T(8,128)S(1)} collective-permute-done((f32[4,66,1]{2,1,0:T(8,128)S(1)}, f32[4,66,1]{2,1,0:T(8,128)S(1)}, u32[]{:S(2)}, u32[]{:S(2)}) %collective-permute-start.13) | collective-permute-done | bytes 1088 | tf_op jit(solution)/shard_map/ppermute | solution.py:14
  104.4 2.0 %collective-permute-start.15 = (f32[4,1,256]{2,1,0:T(1,128)S(1)}, f32[4,1,256]{2,1,0:T(1,128)S(1)}, u32[]{:S(2)}, u32[]{:S(2)}) collective-permute-start(f32[4,1,256]{2,1,0:T(1,128)S(1)} %get-tuple-element.21), channel_id=1, source_target_pairs={{0,4},{4,8},{8,12},{12,16},{16,20},{20,24},{24,28},{28,0},{1,5},{5... | collective-permute-start | bytes 12296 | tf_op jit(solution)/shard_map/ppermute | solution.py:14
  106.4 4.6 %copy.29 = f32[4,64,256]{0,2,1:T(8,128)} copy(f32[4,64,256]{2,1,0:T(8,128)S(1)} %get-tuple-element.10) | data formatting | bytes 524288 | tf_op jit(solution)/shard_map/sub | solution.py:99
  111.0 4.1 %gather_fusion.1 = f32[256,4]{1,0:T(8,128)S(1)} fusion(f32[4,16384]{0,1:T(8,128)} %bitcast.32, s32[1024]{0:T(1024)S(1)} %pad_clamp_fusion), kind=kCustom, calls=%fused_computation.1.clone | custom fusion | bytes 9216 | tf_op jit(solution)/shard_map/jit(_take)/gather | solution.py:82
  117.5 5.1 %scatter_custom_fusion.1 = f32[4,16384]{0,1:T(8,128)} fusion(s32[256]{0:T(256)S(1)} %bitcast.38, f32[256,4]{1,0:T(8,128)S(1)} %copy.31, f32[]{:T(128)} %constant.53.clone.1), kind=kCustom, calls=%fused_computation.4 | custom fusion | flops 1024 | bytes 262148 | tf_op jit(solution)/shard_map/scatter-add | solution.py:85
  122.7 5.2 %copy.32 = f32[4,64,256]{2,1,0:T(8,128)S(1)} copy(f32[4,64,256]{0,2,1:T(8,128)} %bitcast.30) | data formatting | bytes 524288 | tf_op jit(solution)/shard_map/reshape | solution.py:85
  128.3 19.9 %all-reduce = (f32[4]{0:T(128)S(1)}, f32[4]{0:T(128)S(1)}) all-reduce(f32[4]{0:T(128)S(1)} %get-tuple-element.9, f32[4]{0:T(128)S(1)} %fusion.17), channel_id=1, replica_groups=mesh['gx'=8,'gy'=4] {'gx'}, use_global_device_ids=true, to_apply=%region_4.6 | all-reduce | flops 8 | bytes 64 | tf_op jit(solution)/shard_map/psum | solution.py:102
  148.2 5.6 %all-reduce.1 = (f32[4]{0:T(128)S(1)}, f32[4]{0:T(128)S(1)}) all-reduce(f32[4]{0:T(128)S(1)} %get-tuple-element.3, f32[4]{0:T(128)S(1)} %get-tuple-element.4), channel_id=1, replica_groups=mesh['gx'=8,'gy'=4] {'gy'}, use_global_device_ids=true, to_apply=%region_5.7 | all-reduce | flops 8 | bytes 64 | tf_op jit(solution)/shard_map/psum | solution.py:101
  153.8 1.6 multiply_reduce_fusion
  155.4 37.0 %psum.47 = f32[]{:T(128)} all-reduce(f32[]{:T(128)} %get-tuple-element.7), channel_id=1, replica_groups=mesh['gx'=8,'gy'=4] {'gx','gy'}, use_global_device_ids=true, to_apply=%region_11.13 | all-reduce | flops 1 | bytes 8 | tf_op jit(solution)/shard_map/psum | solution.py:115
  (77 shorter events, 13.6 us)
Async XLA Ops:
  0.6 31.1 %copy-start = (f32[1,1,256,256]{3,2,1,0:T(8,128)S(1)}, f32[1,1,256,256]{3,2,1,0:T(8,128)}, u32[]{:S(2)}) copy-start(f32[1,1,256,256]{3,2,1,0:T(8,128)} %param.15) | copy-start | bytes 786436
  0.6 20.5 %copy-start.1 = (f32[64,256]{1,0:T(8,128)S(1)}, f32[64,256]{1,0:T(8,128)}, u32[]{:S(2)}) copy-start(f32[64,256]{1,0:T(8,128)} %param.12) | copy-start | bytes 196612
  0.7 22.6 %copy-start.2 = (f32[64,256]{1,0:T(8,128)S(1)}, f32[64,256]{1,0:T(8,128)}, u32[]{:S(2)}) copy-start(f32[64,256]{1,0:T(8,128)} %param.11) | copy-start | bytes 196612
  0.7 39.3 %copy-start.4 = (s32[1,1,256]{2,1,0:T(1,128)S(1)}, s32[1,1,256]{2,1,0:T(1,128)}, u32[]{:S(2)}) copy-start(s32[1,1,256]{2,1,0:T(1,128)} %param.14) | copy-start | bytes 3076
  0.7 25.9 %copy-start.3 = (f32[64,256]{1,0:T(8,128)S(1)}, f32[64,256]{1,0:T(8,128)}, u32[]{:S(2)}) copy-start(f32[64,256]{1,0:T(8,128)} %param.10) | copy-start | bytes 196612
  1.8 19.5 %collective-permute-start = (f32[4,1,256]{2,1,0:T(1,128)S(1)}, f32[4,1,256]{2,1,0:T(1,128)S(1)}, u32[]{:S(2)}, u32[]{:S(2)}) collective-permute-start(f32[4,1,256]{2,1,0:T(1,128)S(1)} %get-tuple-element.28), channel_id=1, source_target_pairs={{4,0},{8,4},{12,8},{16,12},{20,16},{24,20},{28,24},{0,28},{5,1},{9... | collective-permute-start | bytes 12296 | tf_op jit(solution)/shard_map/ppermute | solution.py:16
  7.8 13.4 %collective-permute-start.2 = (f32[4,1,256]{2,1,0:T(1,128)S(1)}, f32[4,1,256]{2,1,0:T(1,128)S(1)}, u32[]{:S(2)}, u32[]{:S(2)}) collective-permute-start(f32[4,1,256]{2,1,0:T(1,128)S(1)} %get-tuple-element.27), channel_id=1, source_target_pairs={{0,4},{4,8},{8,12},{12,16},{16,20},{20,24},{24,28},{28,0},{1,5},{5... | collective-permute-start | bytes 12296 | tf_op jit(solution)/shard_map/ppermute | solution.py:14
  8.6 12.5 %collective-permute-start.4 = (f32[64,1]{1,0:T(8,128)S(1)}, f32[64,1]{1,0:T(8,128)S(1)}, u32[]{:S(2)}, u32[]{:S(2)}) collective-permute-start(f32[64,1]{1,0:T(8,128)S(1)} %slice.138), channel_id=1, source_target_pairs={{0,1},{1,2},{2,3},{3,0},{4,5},{5,6},{6,7},{7,4},{8,9},{9,10},{10,1... | collective-permute-start | bytes 776 | tf_op jit(solution)/shard_map/ppermute | solution.py:26
  9.4 13.9 %collective-permute-start.1 = (f32[1,256]{1,0:T(1,128)S(1)}, f32[1,256]{1,0:T(1,128)S(1)}, u32[]{:S(2)}, u32[]{:S(2)}) collective-permute-start(f32[1,256]{1,0:T(1,128)S(1)} %slice.132), channel_id=1, source_target_pairs={{0,4},{4,8},{8,12},{12,16},{16,20},{20,24},{24,28},{28,0},{1,5},{5... | collective-permute-start | bytes 3080 | tf_op jit(solution)/shard_map/ppermute | solution.py:26
  21.4 4.6 %collective-permute-start.5 = (f32[4,66,1]{2,1,0:T(8,128)S(1)}, f32[4,66,1]{2,1,0:T(8,128)S(1)}, u32[]{:S(2)}, u32[]{:S(2)}) collective-permute-start(f32[4,66,1]{2,1,0:T(8,128)S(1)} %get-tuple-element.20), channel_id=1, source_target_pairs={{0,1},{1,2},{2,3},{3,0},{4,5},{5,6},{6,7},{7,4},{8,9},{9,10},{10,1... | collective-permute-start | bytes 3176 | tf_op jit(solution)/shard_map/ppermute | solution.py:14
  23.1 3.6 %collective-permute-start.3 = (f32[4,66,1]{2,1,0:T(8,128)S(1)}, f32[4,66,1]{2,1,0:T(8,128)S(1)}, u32[]{:S(2)}, u32[]{:S(2)}) collective-permute-start(f32[4,66,1]{2,1,0:T(8,128)S(1)} %get-tuple-element.19), channel_id=1, source_target_pairs={{1,0},{2,1},{3,2},{0,3},{5,4},{6,5},{7,6},{4,7},{9,8},{10,9},{11,1... | collective-permute-start | bytes 3176 | tf_op jit(solution)/shard_map/ppermute | solution.py:16
  26.9 6.1 %collective-permute-start.6 = (f32[4,1,256]{2,1,0:T(1,128)S(1)}, f32[4,1,256]{2,1,0:T(1,128)S(1)}, u32[]{:S(2)}, u32[]{:S(2)}) collective-permute-start(f32[4,1,256]{2,1,0:T(1,128)S(1)} %get-tuple-element.26), channel_id=1, source_target_pairs={{4,0},{8,4},{12,8},{16,12},{20,16},{24,20},{28,24},{0,28},{5,1},{9... | collective-permute-start | bytes 12296 | tf_op jit(solution)/shard_map/ppermute | solution.py:16
  31.7 6.3 %collective-permute-start.7 = (f32[4,1,256]{2,1,0:T(1,128)S(1)}, f32[4,1,256]{2,1,0:T(1,128)S(1)}, u32[]{:S(2)}, u32[]{:S(2)}) collective-permute-start(f32[4,1,256]{2,1,0:T(1,128)S(1)} %get-tuple-element.25), channel_id=1, source_target_pairs={{0,4},{4,8},{8,12},{12,16},{16,20},{20,24},{24,28},{28,0},{1,5},{5... | collective-permute-start | bytes 12296 | tf_op jit(solution)/shard_map/ppermute | solution.py:14
  38.1 12.3 %collective-permute-start.9 = (f32[4,66,1]{2,1,0:T(8,128)S(1)}, f32[4,66,1]{2,1,0:T(8,128)S(1)}, u32[]{:S(2)}, u32[]{:S(2)}) collective-permute-start(f32[4,66,1]{2,1,0:T(8,128)S(1)} %get-tuple-element.18), channel_id=1, source_target_pairs={{0,1},{1,2},{2,3},{3,0},{4,5},{5,6},{6,7},{7,4},{8,9},{9,10},{10,1... | collective-permute-start | bytes 3176 | tf_op jit(solution)/shard_map/ppermute | solution.py:14
  38.2 12.3 %collective-permute-start.8 = (f32[4,66,1]{2,1,0:T(8,128)S(1)}, f32[4,66,1]{2,1,0:T(8,128)S(1)}, u32[]{:S(2)}, u32[]{:S(2)}) collective-permute-start(f32[4,66,1]{2,1,0:T(8,128)S(1)} %get-tuple-element.17), channel_id=1, source_target_pairs={{1,0},{2,1},{3,2},{0,3},{5,4},{6,5},{7,6},{4,7},{9,8},{10,9},{11,1... | collective-permute-start | bytes 3176 | tf_op jit(solution)/shard_map/ppermute | solution.py:16
  88.2 5.4 %collective-permute-start.10 = (f32[4,1,256]{2,1,0:T(1,128)S(1)}, f32[4,1,256]{2,1,0:T(1,128)S(1)}, u32[]{:S(2)}, u32[]{:S(2)}) collective-permute-start(f32[4,1,256]{2,1,0:T(1,128)S(1)} %get-tuple-element.24), channel_id=1, source_target_pairs={{4,0},{8,4},{12,8},{16,12},{20,16},{24,20},{28,24},{0,28},{5,1},{9... | collective-permute-start | bytes 12296 | tf_op jit(solution)/shard_map/ppermute | solution.py:16
  92.3 6.3 %collective-permute-start.11 = (f32[4,1,256]{2,1,0:T(1,128)S(1)}, f32[4,1,256]{2,1,0:T(1,128)S(1)}, u32[]{:S(2)}, u32[]{:S(2)}) collective-permute-start(f32[4,1,256]{2,1,0:T(1,128)S(1)} %get-tuple-element.23), channel_id=1, source_target_pairs={{0,4},{4,8},{8,12},{12,16},{16,20},{20,24},{24,28},{28,0},{1,5},{5... | collective-permute-start | bytes 12296 | tf_op jit(solution)/shard_map/ppermute | solution.py:14
  98.7 4.6 %collective-permute-start.13 = (f32[4,66,1]{2,1,0:T(8,128)S(1)}, f32[4,66,1]{2,1,0:T(8,128)S(1)}, u32[]{:S(2)}, u32[]{:S(2)}) collective-permute-start(f32[4,66,1]{2,1,0:T(8,128)S(1)} %get-tuple-element.16), channel_id=1, source_target_pairs={{0,1},{1,2},{2,3},{3,0},{4,5},{5,6},{6,7},{7,4},{8,9},{9,10},{10,1... | collective-permute-start | bytes 3176 | tf_op jit(solution)/shard_map/ppermute | solution.py:14
  98.8 5.2 %collective-permute-start.12 = (f32[4,66,1]{2,1,0:T(8,128)S(1)}, f32[4,66,1]{2,1,0:T(8,128)S(1)}, u32[]{:S(2)}, u32[]{:S(2)}) collective-permute-start(f32[4,66,1]{2,1,0:T(8,128)S(1)} %get-tuple-element.15), channel_id=1, source_target_pairs={{1,0},{2,1},{3,2},{0,3},{5,4},{6,5},{7,6},{4,7},{9,8},{10,9},{11,1... | collective-permute-start | bytes 3176 | tf_op jit(solution)/shard_map/ppermute | solution.py:16
  104.3 10.9 %collective-permute-start.14 = (f32[4,1,256]{2,1,0:T(1,128)S(1)}, f32[4,1,256]{2,1,0:T(1,128)S(1)}, u32[]{:S(2)}, u32[]{:S(2)}) collective-permute-start(f32[4,1,256]{2,1,0:T(1,128)S(1)} %get-tuple-element.22), channel_id=1, source_target_pairs={{4,0},{8,4},{12,8},{16,12},{20,16},{24,20},{28,24},{0,28},{5,1},{9... | collective-permute-start | bytes 12296 | tf_op jit(solution)/shard_map/ppermute | solution.py:16
  104.4 10.8 %collective-permute-start.15 = (f32[4,1,256]{2,1,0:T(1,128)S(1)}, f32[4,1,256]{2,1,0:T(1,128)S(1)}, u32[]{:S(2)}, u32[]{:S(2)}) collective-permute-start(f32[4,1,256]{2,1,0:T(1,128)S(1)} %get-tuple-element.21), channel_id=1, source_target_pairs={{0,4},{4,8},{8,12},{12,16},{16,20},{20,24},{24,28},{28,0},{1,5},{5... | collective-permute-start | bytes 12296 | tf_op jit(solution)/shard_map/ppermute | solution.py:14
  115.3 12.6 %collective-permute-start.17 = (f32[4,66,1]{2,1,0:T(8,128)S(1)}, f32[4,66,1]{2,1,0:T(8,128)S(1)}, u32[]{:S(2)}, u32[]{:S(2)}) collective-permute-start(f32[4,66,1]{2,1,0:T(8,128)S(1)} %get-tuple-element.14), channel_id=1, source_target_pairs={{0,1},{1,2},{2,3},{3,0},{4,5},{5,6},{6,7},{7,4},{8,9},{9,10},{10,1... | collective-permute-start | bytes 3176 | tf_op jit(solution)/shard_map/ppermute | solution.py:14
  115.8 12.1 %collective-permute-start.16 = (f32[4,66,1]{2,1,0:T(8,128)S(1)}, f32[4,66,1]{2,1,0:T(8,128)S(1)}, u32[]{:S(2)}, u32[]{:S(2)}) collective-permute-start(f32[4,66,1]{2,1,0:T(8,128)S(1)} %get-tuple-element.13), channel_id=1, source_target_pairs={{1,0},{2,1},{3,2},{0,3},{5,4},{6,5},{7,6},{4,7},{9,8},{10,9},{11,1... | collective-permute-start | bytes 3176 | tf_op jit(solution)/shard_map/ppermute | solution.py:16
